TPU v7x, 512 devices: a whole 4x4x16 slice. The times are simulated.
512 devices in a mesh: rep: 8 (over x_hi, y), grp: 64 (over x_lo, z, core).
Axes of the slice: x: 4 (x_hi: 2, x_lo: 2; x = x_hi * 2 + x_lo), y: 4, z: 16, core: 2. Of those that a mesh axis runs over, the one named last changes fastest.
Arguments:
- layer_inputs: bfloat16 [16384, 3584], P('grp'), may hold values from -32 to 32
- loss_adjoint_matrix: bfloat16 [16384, 3584], P('grp'), may hold values from -0.1875 to 0.1875
- attention_projection_matrix: bfloat16 [3584, 768], P(('rep', 'grp')), may hold values from -0.09375 to 0.09375
- merge_projection_transposed: bfloat16 [3584, 512], P(('rep', 'grp')), may hold values from -0.25 to 0.25
- packed_sequence_labels: int32 [64, 256], P('grp'), may hold values from 0 to 3, never falling along the last dimension, each value on 1 to 128 neighbouring positions
- dropout_factors: bfloat16 [8, 16384, 4, 256], P('rep', 'grp'), may hold values from -0.75 to 0.75
- straggler_filter: int32 [8, 64], P(None, 'grp'), may hold values from 0 to 1, as said below
Outputs:
- gradient: float32 [3584, 1280], P(('rep', 'grp'))
Inputs may be any that keep to these rules, and one draw needn't show every extreme that they name: `straggler_filter`: each column (partition) holds exactly one 1, the surviving replica; all other entries are 0.
All inputs are finite; a program needn't handle non-finite values.
Results may differ from a plain program's by a relative error of at most 0.008.
The roundings to bfloat16 on the way count: a program that leaves them out, or rounds other values in their place, can miss the bound.
Values may be sent and summed in bfloat16 or wider, within the bound.
A program may use at most 64 MiB of HBM per device.

v0:
```python
import jax
import jax.numpy as jnp
from jax import lax
from jax.sharding import Mesh
from jax.sharding import PartitionSpec as P

REP = ("rep_0", "rep_1")
REP_GRP = ("rep_0", "rep_1", "grp")


def in_one_piece(arrays, axis, dim, along):
    both = jnp.concatenate(arrays, axis=along)
    filled, at, gathered = (lax.all_gather(both, axis, axis=dim, tiled=True), 0, [])
    for a in arrays:
        gathered.append(lax.slice_in_dim(filled, at, at + a.shape[along], axis=along))
        at += a.shape[along]
    return tuple(gathered)


def in_one(arrays, axis):
    ends = [0]
    for a in arrays:
        ends.append(ends[-1] + a.size)
    total = lax.psum(jnp.concatenate([a.ravel() for a in arrays]), axis)
    return tuple((total[b:e].reshape(a.shape) for a, b, e in zip(arrays, ends, ends[1:])))


def from_root(value, axes, root):
    value = jnp.where(lax.axis_index(axes) == root, value, jnp.zeros_like(value))
    for axis in axes:
        value = lax.psum(value, axis)
    return value


def cut_along(value, dim, devices):
    lengths = value.shape
    tiles = value.reshape(*lengths[:dim], devices, lengths[dim] // devices, *lengths[dim + 1 :])
    return jnp.moveaxis(tiles, dim, 0)


def sent_and_summed(value, axis, dim):
    devices = lax.axis_size(axis)
    tiles = lax.all_to_all(cut_along(value, dim, devices), axis, 0, 0, tiled=True)
    return jnp.sum(tiles.astype(jnp.float32), axis=0)


def token_grads(projected_wide, attn_wide, doc_row, noise_rows):
    seq_len = projected_wide.shape[0]
    head_size = (projected_wide.shape[1] - attn_wide.shape[1]) // 2
    heads = attn_wide.shape[1] // head_size
    score_scale = 1.0 / jnp.sqrt(jnp.float32(head_size))
    projected = projected_wide.astype(jnp.bfloat16)
    queries = projected[:, : heads * head_size]
    key_rows = projected[:, heads * head_size : (heads + 1) * head_size]
    val_rows = projected[:, (heads + 1) * head_size :]
    query_heads = queries.reshape(seq_len, heads, head_size).astype(jnp.float32)
    keys_wide = key_rows.astype(jnp.float32)
    vals_wide = val_rows.astype(jnp.float32)
    position = jnp.arange(seq_len, dtype=jnp.int32)
    allowed = (doc_row[:, None] == doc_row[None, :]) & (position[None, :] <= position[:, None])
    scores = jnp.einsum("ihd,jd->hij", query_heads, keys_wide) * score_scale
    scores = jnp.where(allowed[None], scores, -jnp.inf)
    highest = jnp.max(scores, axis=2, keepdims=True)
    expon = jnp.exp(scores - highest)
    attn_probs = expon / jnp.sum(expon, axis=2, keepdims=True)
    factor = 1.0 + jnp.transpose(noise_rows.astype(jnp.float32), (1, 0, 2))
    dropped = (attn_probs * factor).astype(jnp.bfloat16)
    dropped_wide = dropped.astype(jnp.float32)
    attended = (
        jnp.einsum("hij,jd->ihd", dropped_wide, vals_wide)
        .astype(jnp.bfloat16)
        .reshape(seq_len, heads * head_size)
    )
    attn_grad = attn_wide.astype(jnp.bfloat16)
    grad_heads = attn_grad.reshape(seq_len, heads, head_size).astype(jnp.float32)
    val_grad = jnp.einsum("hij,ihd->jd", dropped_wide, grad_heads).astype(jnp.bfloat16)
    prob_grad = jnp.einsum("ihd,jd->hij", grad_heads, vals_wide) * factor
    inner = jnp.sum(attn_probs * prob_grad, axis=2, keepdims=True)
    score_grad = (attn_probs * (prob_grad - inner) * score_scale).astype(jnp.bfloat16)
    score_wide = score_grad.astype(jnp.float32)
    query_grad = (
        jnp.einsum("hij,jd->ihd", score_wide, keys_wide)
        .astype(jnp.bfloat16)
        .reshape(seq_len, heads * head_size)
    )
    key_grad = jnp.einsum("hij,ihd->jd", score_wide, query_heads).astype(jnp.bfloat16)
    stacked = jnp.concatenate([query_grad, key_grad, val_grad], axis=1)
    return (stacked, attended)


def weight_rows(hidden_rows, cot_rows, stacked, attended, first_row, row_count):
    hidden_cols = lax.dynamic_slice_in_dim(hidden_rows, first_row, row_count, 1)
    cot_cols = lax.dynamic_slice_in_dim(cot_rows, first_row, row_count, 1)
    proj_grad = jnp.dot(hidden_cols.T, stacked, preferred_element_type=jnp.float32)
    out_grad = jnp.dot(cot_cols.T, attended, preferred_element_type=jnp.float32)
    return jnp.concatenate([proj_grad, out_grad], axis=1)


def per_device(
    layer_inputs,
    loss_adjoint_matrix,
    attention_projection_matrix,
    merge_projection_transposed,
    packed_sequence_labels,
    dropout_factors,
    straggler_filter,
):
    duplicate_workers = lax.axis_size(REP)
    member = lax.axis_index(REP)
    kept_worker = jnp.sum(jnp.arange(duplicate_workers, dtype=jnp.int32) * straggler_filter[:, 0])
    row_count = layer_inputs.shape[1] // duplicate_workers
    first_row = member * row_count
    qkv_part, out_part = in_one_piece(
        (attention_projection_matrix, merge_projection_transposed), "grp", 0, 1
    )
    hidden_cols = lax.dynamic_slice_in_dim(layer_inputs, first_row, row_count, 1)
    cot_cols = lax.dynamic_slice_in_dim(loss_adjoint_matrix, first_row, row_count, 1)
    part_proj = jnp.dot(hidden_cols, qkv_part, preferred_element_type=jnp.float32)
    part_attn = jnp.dot(cot_cols, out_part, preferred_element_type=jnp.float32)
    projected_wide, attn_wide = in_one((part_proj, part_attn), REP)
    chosen_noise = from_root(dropout_factors[0], REP, kept_worker)
    stacked, attended = token_grads(
        projected_wide, attn_wide, packed_sequence_labels[0], chosen_noise
    )
    gradient = weight_rows(
        layer_inputs, loss_adjoint_matrix, stacked, attended, first_row, row_count
    )
    return sent_and_summed(gradient.astype(jnp.bfloat16), "grp", 0)


def solution(mesh):
    torus = Mesh(mesh.devices.reshape(2, 4, mesh.shape["grp"]), ("rep_0", "rep_1", "grp"))
    return jax.shard_map(
        per_device,
        mesh=torus,
        in_specs=(
            P("grp", None),
            P("grp", None),
            P(REP_GRP, None),
            P(REP_GRP, None),
            P("grp", None),
            P(REP, "grp", None, None),
            P(None, "grp"),
        ),
        out_specs=P(REP_GRP, None),
        check_vma=False,
    )
```

profile of v0, /device:TPU:24, one launch (start us, length us, event | category | flops | bytes accessed | tf_op | source)
XLA Modules:
  0.0 327.0 jit_solution(6663240458485747039)
XLA Ops:
  7.4 0.0 copy-start
  7.4 0.0 all-reduce.4.cloned.1.call-start
  7.4 1.4 fusion.34
  8.8 0.0 copy-start.5
  8.8 0.0 copy-start.6
  8.8 1.3 copy.30
  10.8 0.8 select_bitcast_fusion
  11.6 0.0 copy-start.7
  11.7 0.0 all-reduce.4.cloned.1.call-update
  11.7 0.0 all-gather.3.cloned.1.call-start
  11.7 0.0 copy-done.5
  11.7 0.0 copy-done.6
  11.7 0.6 maximum_bitcast_fusion
  12.4 0.0 all-gather.3.cloned.1.call-update
  12.4 0.0 all-reduce.6.cloned.1.call-start
  12.4 1.1 dynamic-slice_bitcast_fusion
  13.6 0.1 copy.36
  13.7 0.8 dot_general.43
  14.5 0.0 copy-done.7
  14.5 0.7 fusion.28
  15.2 53.3 %all-reduce.4.cloned.1.call-done = bf16[256,4,256]{0,2,1:T(8,128)(2,1)} async-done(((bf16[256,4,256]{0,2,1:T(8,128)(2,1)}), bf16[256,4,256]{0,2,1:T(8,128)(2,1)}) %all-reduce.4.cloned.1.call-update) | async-done | bytes 524304 | tf_op jit(solution)/shard_map/psum | solution.py:31
  68.5 0.0 all-reduce.6.cloned.1.call-update
  68.6 71.5 %all-gather.3.cloned.1.call-done = bf16[64,7,1280]{2,1,0:T(8,128)(2,1)} async-done(((bf16[1,7,1280]{2,1,0:T(8,128)(2,1)}), bf16[64,7,1280]{2,1,0:T(8,128)(2,1)}) %all-gather.3.cloned.1.call-update) | async-done | bytes 1146896 | tf_op jit(solution)/shard_map/all_gather | solution.py:13
  140.1 1.5 reshape.92
  141.6 1.3 convolution_bitcast_fusion.1
  142.9 0.0 copy-done
  142.9 1.3 fusion.18
  144.2 2.1 reshape.85
  146.3 0.0 copy-start.1
  146.3 0.1 copy.53
  146.5 1.0 copy-done.1
  147.4 0.1 pad_maximum_fusion
  147.5 78.7 %all-reduce.7 = bf16[327680]{0:T(1024)(128)(2,1)} all-reduce(f32[327680]{0:T(1024)S(1)} %pad_maximum_fusion), channel_id=1, replica_groups=mesh['rep_0'=2,'rep_1'=4,'grp'=64] {'rep_0','rep_1'}, use_global_device_ids=true, to_apply=%region_0.0 | all-reduce | flops 327680 | bytes 1966080 | tf_op jit(solution)/shard_map/psum | solution.py:24
  226.2 0.0 slice-start
  226.2 0.0 slice-start.1
  226.2 1.0 slice-done
  227.2 0.0 copy-start.4
  227.2 0.4 convert_element_type.44
  227.6 0.0 slice-done.1
  227.6 0.2 copy.35
  227.8 0.1 copy.27
  227.9 0.1 copy-done.4
  228.1 1.4 fusion.47
  229.5 0.0 all-reduce.6.cloned.1.call-done
  229.5 2.4 fusion.7
  231.9 3.4 %convolution_convert_fusion.3 = bf16[128,4,256]{2,0,1:T(8,128)(2,1)} fusion(f32[4,256,256]{1,2,0:T(8,128)} %fusion.7, bf16[256,768]{1,0:T(8,128)(2,1)S(1)} %convert_element_type.44, f32[4,256,256]{1,2,0:T(8,128)} %get-tuple-element.6, f32[4,256]{1,0:T(4,128)S(1)} %get-tuple-element.5), kind=kOutput, calls=%fused_computation.20 | convolution fusion | flops 69076224 | bytes 4530176 | tf_op jit(solution)/shard_map/hij,jd->ihd/dot_general | solution.py:82
  235.3 0.0 copy-start.3
  235.3 2.7 fusion.11
  237.9 0.0 copy-done.3
  238.0 0.8 fusion.12
  238.8 2.4 convolution_convert_fusion
  241.2 1.3 concatenate.19
  242.5 0.0 copy-start.2
  242.5 2.6 convolution_convert_fusion.2
  245.1 0.0 copy-done.2
  245.1 1.3 convolution_convert_fusion.1
  246.4 0.3 copy.41
  246.6 0.2 pad_maximum_fusion.1
  246.8 71.8 %all_to_all.5 = bf16[64,7,1280]{2,1,0:T(8,128)(2,1)S(1)} all-to-all(bf16[64,7,1280]{2,1,0:T(8,128)(2,1)S(1)} %pad_maximum_fusion.1), channel_id=1, replica_groups=mesh['rep_0'=2,'rep_1'=4,'grp'=64] {'grp'}, dimensions={0} | all-to-all | bytes 2293760 | tf_op jit(solution)/shard_map/all_to_all | solution.py:43
  318.7 0.9 convert_reduce_fusion
  (1 shorter events, 0.0 us)
Async XLA Ops:
  7.4 135.5 %copy-start = (bf16[256,3584]{1,0:T(8,128)(2,1)S(1)}, bf16[256,3584]{1,0:T(8,128)(2,1)}, u32[]{:S(2)}) copy-start(bf16[256,3584]{1,0:T(8,128)(2,1)} %param.7) | copy-start | bytes 5505028
  7.4 61.2 %all-reduce.4.cloned.1.call-start = ((), (), s32[]{:S(2)}) async-start(), calls=%async_computation.1 | async-start | bytes 1048576 | tf_op jit(solution)/shard_map/psum | solution.py:31
  8.8 2.9 copy-start.5
  8.8 2.9 copy-start.6
  11.6 2.8 copy-start.7
  11.7 128.4 %all-gather.3.cloned.1.call-start = ((), (), s32[]{:S(2)}) async-start(), calls=%async_computation.3 | async-start | bytes 1331200 | tf_op jit(solution)/shard_map/all_gather | solution.py:13
  12.4 217.1 %all-reduce.6.cloned.1.call-start = ((), (), s32[]{:S(2)}) async-start(), calls=%async_computation.2 | async-start | bytes 1048576 | tf_op jit(solution)/shard_map/psum | solution.py:31
  146.3 1.1 copy-start.1
  226.2 1.0 slice-start
  226.2 1.4 slice-start.1
  227.2 0.9 copy-start.4
  235.3 2.7 copy-start.3
  242.5 2.6 copy-start.2
Sparse Core Ops, SparseCore 0:
  11.8 56.6 all-reduce.3
  70.9 56.5 all-reduce.5
Sparse Core Ops, SparseCore 1:
  14.3 125.7 all-gather.2
where the time goes:
time: 332 us; the launch traced here: 327 us
  blocking collectives  150 us (45%)
  waiting for transfers between devices  125 us (38%)
  matrix products  19.5 us (6%)
  between operations  15.7 us (5%)
  local copies, waits for them, and re-layouts  11.5 us (3%)
  other arithmetic  4.81 us (1%)
    psum x1, blocking collectives, in_one(): total = lax.psum(jnp.concatenate([a.ravel() for a in arrays]), axis)  78.7 us
    all_to_all x1, blocking collectives, sent_and_summed(): lax.all_to_all(cut_along(value, dim, devices), axis, 0, 0, tiled=True)  71.8 us
    all_gather x1, waiting for transfers between devices, in_one_piece(): lax.all_gather(both, axis, axis=dim, tiled=True)  71.5 us
    psum x2, waiting for transfers between devices, from_root(): value = lax.psum(value, axis)  53.3 us
  transfers between devices with their start and end apart: 3, of which 2 were waited for; matrix products, arithmetic and copies ran while one was open for 4% of the time, Pallas kernels for 0%

commit v1 on v0

v1 whole, which is shorter than its diff:
```python
import functools

import jax
import jax.numpy as jnp
from jax import lax
from jax.experimental import pallas as pl
from jax.experimental.pallas import tpu as pltpu
from jax.sharding import PartitionSpec as P

MESH = pl.DeviceIdType.MESH
BF = jnp.bfloat16
F32 = jnp.float32
REPS = 8
NZ = 16
PIECES = 64
REACH = 4
SEQ = 256
D = 3584
HD = 128
HQ = 4
ROWS = 7
OUTC = 1280


def iota(shape, dim):
    return lax.broadcasted_iota(jnp.int32, shape, dim)


def dot(a, b, dims=((1,), (0,))):
    return lax.dot_general(a, b, (dims, ((), ())), preferred_element_type=F32)


def kernel(
    x_hbm, y_hbm, wqkv_ref, wo_ref, lab_ref, noise_hbm, filt_ref,
    out_ref,
    xb, zb, yw, sel_e, own_e, xe, ze, xo_t, yo_t, p0s, p0r, wbuf,
    nrecv, nstage, nfull, prj, kv_ref, g32, gs, r1, s2, r2, acc, s3, relay, fin, allow,
    loc, p0_send, p0_recv, nz_send, nz_recv, nf_send, nf_recv, w_send, w_recv,
    pr_send, pr_recv, r1_send, r1_recv, r2_send, r2_recv, r3_send, relay_recv, fin_recv,
):
    rep = lax.axis_index("rep")
    grp = lax.axis_index("grp")
    x_lo = grp // 32
    z = (grp // 2) % NZ
    core = grp % 2
    partner = grp + 1 - 2 * core
    beside = grp + 32 - 64 * x_lo

    def along(d):
        return lax.rem(z + (d + NZ), NZ)

    def at_z(zz):
        return x_lo * 32 + zz * 2 + core

    def rcopy(src, dst, ssem, rsem, r, g):
        return pltpu.make_async_remote_copy(
            src_ref=src, dst_ref=dst, send_sem=ssem, recv_sem=rsem,
            device_id=(r, g), device_id_type=MESH,
        )

    def mate(k):
        return lax.rem(rep + k, REPS)

    barrier = pltpu.get_barrier_semaphore()
    near = [d for s in range(1, REACH + 1) for d in (s, -s)]
    for d in near:
        pl.semaphore_signal(barrier, inc=1, device_id=(rep, at_z(along(d))), device_id_type=MESH)
    for k in range(1, REPS):
        pl.semaphore_signal(barrier, inc=1, device_id=(mate(k), grp), device_id_type=MESH)
    pl.semaphore_signal(barrier, inc=1, device_id=(rep, partner), device_id_type=MESH)
    pl.semaphore_signal(barrier, inc=1, device_id=(rep, beside), device_id_type=MESH)

    window = pl.multiple_of(128 * (3 * rep + rep // 2), 128)
    shift_own = 64 * (rep % 2)
    cx = pltpu.make_async_copy(x_hbm, xb, loc.at[0])
    cx.start()
    czx = pltpu.make_async_copy(x_hbm, zb, loc.at[1])
    czy = pltpu.make_async_copy(y_hbm, zb, loc.at[1])

    @pl.when(rep < HQ)
    def _():
        czx.start()

    @pl.when(rep >= HQ)
    def _():
        czy.start()

    cy = pltpu.make_async_copy(y_hbm.at[:, pl.ds(window, 512)], yw, loc.at[2])
    cy.start()
    cn = pltpu.make_async_copy(
        noise_hbm.at[0, pl.ds(rep * 32, 32)], nrecv.at[rep], loc.at[3]
    )
    cn.start()

    zero_row = jnp.zeros((1, 768), F32)
    wq = jnp.concatenate([wqkv_ref[...].astype(F32), zero_row], axis=0)
    wo = jnp.concatenate([wo_ref[...].astype(F32), zero_row[:, :512]], axis=0)
    lane8 = iota((8, 128), 1)
    slot = rep // 2
    for d in range(REPS):
        if d < HQ:
            chunk, kv = wq[:, 128 * d : 128 * d + 128], wq[:, 512:640]
        else:
            chunk, kv = wo[:, 128 * (d - HQ) : 128 * (d - HQ) + 128], wq[:, 640:768]
        turned = pltpu.roll(kv, lax.rem(32 * slot + 128 - 32 * (d % 4), 128), 1)
        p0s[d, 0] = chunk.astype(BF)
        p0s[d, 1] = jnp.where(lane8 // 32 == slot, turned, 0.0).astype(BF)
    p0r[rep] = p0s[rep]

    pl.semaphore_wait(barrier, len(near) + REPS - 1 + 2)

    for k in range(1, REPS):
        rcopy(p0s.at[mate(k)], p0r.at[rep], p0_send, p0_recv.at[rep], mate(k), grp).start()
    for k in range(1, REPS):
        m = mate(k)
        rcopy(
            noise_hbm.at[0, pl.ds(m * 32, 32)], nrecv.at[rep], nz_send, nz_recv.at[rep], m, grp
        ).start()

    col = iota((128, 1024), 1)
    part = col % 16
    target = 448 * (part // 8) + 7 * (col // 16) + part % 8
    target = jnp.where(part % 8 < ROWS, target, -1)

    def fill_e(b, carry):
        sel_e[pl.ds(pl.multiple_of(128 * b, 128), 128), :] = jnp.where(
            iota((128, 1024), 0) + 128 * b == target, 1.0, 0.0
        ).astype(BF)
        return carry

    lax.fori_loop(0, 7, fill_e, 0)

    for k in range(1, REPS):
        s = mate(k)
        rcopy(p0s.at[s], p0r.at[s], p0_send, p0_recv.at[s], s, grp).wait_recv()
    for t in range(4):
        wbuf[t, grp, 0:8] = p0r[2 * t, 0]
        wbuf[t, grp, 8:16] = p0r[2 * t + 1, 0]
    for half in range(2):
        total = p0r[half, 1].astype(F32)
        for b in range(1, 4):
            total = total + p0r[2 * b + half, 1].astype(F32)
        wbuf[4, grp, 8 * half : 8 * half + 8] = total.astype(BF)

    def piece(p, g):
        return rcopy(wbuf.at[:, p], wbuf.at[:, p], w_send, w_recv.at[p], rep, g)

    for s in range(REACH, 0, -1):
        piece(grp, at_z(along(s))).start()
        piece(grp, at_z(along(-s))).start()
    piece(grp, beside).start()
    piece(grp, partner).start()

    cx.wait()
    czx.wait()

    def spread(t, carry):
        lanes = pl.ds(pl.multiple_of(896 * t, 128), 896)
        xe[t] = dot(xb[:, lanes], sel_e[...]).astype(BF)
        ze[t] = dot(zb[:, lanes], sel_e[...]).astype(BF)
        return carry

    def land(d):
        p = at_z(along(d))
        piece(p, grp).wait_recv()
        return p

    def hand_on(p):
        piece(p, beside).start()
        piece(p, partner).start()

    lax.fori_loop(0, 2, spread, 0)

    p = land(-REACH)
    for s in range(REACH, 0, -1):
        piece(p, at_z(along(s))).start()
    hand_on(p)
    p = land(REACH)
    for s in range(REACH - 1, 0, -1):
        piece(p, at_z(along(-s))).start()
    hand_on(p)
    for s in range(REACH - 1, 0, -1):
        hand_on(land(-s))
        hand_on(land(s))

    cn.wait()
    for k in range(1, REPS):
        s = mate(k)
        rcopy(
            noise_hbm.at[0, pl.ds(s * 32, 32)], nrecv.at[s], nz_send, nz_recv.at[s], s, grp
        ).wait_recv()
    kept = nrecv[0].astype(F32)
    for s in range(1, REPS):
        kept = jnp.where(filt_ref[0, s] == 1, nrecv[s].astype(F32), kept)
    for h in range(HQ):
        nstage[h] = kept[:, h, :].astype(BF)
    rows_own = pl.ds(pl.multiple_of(rep * 32, 32), 32)
    for h in range(HQ):
        nfull[h, rows_own] = nstage[h]
    for k in range(1, REPS):
        rcopy(nstage, nfull.at[:, rows_own], nf_send, nf_recv.at[rep], mate(k), grp).start()

    lax.fori_loop(2, 4, spread, 0)

    for s in range(REACH + 1, 2 * REACH):
        hand_on(land(-s))
        hand_on(land(s))
    hand_on(land(-2 * REACH))

    crow = iota((512, 128), 0)
    pidx = crow // 8
    owner = ((pidx // 16) % 2) * 32 + (pidx % 16) * 2 + pidx // 32
    want = shift_own + 7 * owner + crow % 8
    want = jnp.where(crow % 8 < ROWS, want, -1)
    for b in range(4):
        own_e[:, 128 * b : 128 * b + 128] = jnp.where(
            iota((512, 128), 1) + 128 * b == want, 1.0, 0.0
        ).astype(BF)
    cy.wait()
    xo_t[...] = dot(own_e[...], xb[:, pl.ds(window, 512)], ((1,), (1,))).astype(BF)
    yo_t[...] = dot(own_e[...], yw[...], ((1,), (1,))).astype(BF)

    lab = lab_ref[...]
    qi, kj = iota((SEQ, SEQ), 0), iota((SEQ, SEQ), 1)
    lab_col = jnp.sum(jnp.where(qi == kj, lab, 0), axis=1, keepdims=True)
    allow[...] = jnp.where((lab_col == lab) & (kj <= qi), 1.0, 0.0)

    def from_beside(i, carry):
        zz = lax.rem(z + i, NZ)
        q = (1 - x_lo) * 32 + zz * 2 + core
        piece(q, grp).wait_recv()
        piece(q, partner).start()
        return carry

    lax.fori_loop(0, NZ, from_beside, 0)

    def from_partner(i, carry):
        zz = lax.rem(z + i, NZ)
        piece(zz * 2 + 1 - core, grp).wait_recv()
        piece(32 + zz * 2 + 1 - core, grp).wait_recv()
        return carry

    lax.fori_loop(0, NZ, from_partner, 0)

    own_cols = jnp.zeros((SEQ, HD), F32)
    for t in range(4):
        own_cols = own_cols + dot(ze[t], wbuf[t].reshape(1024, HD))
    lane = iota((SEQ, HD), 1) // 32
    kv_sum = jnp.zeros((SEQ, HD), F32)
    w_kv = wbuf[4].reshape(1024, HD)
    for b in range(4):
        kv_sum = jnp.where(lane == b, dot(xe[b], w_kv), kv_sum)
    kv_sum = kv_sum + pltpu.roll(kv_sum, 64, 1)
    kv_sum = kv_sum + pltpu.roll(kv_sum, 32, 1)
    lane64 = iota((64, HD), 1) // 32
    packed = kv_sum[0:64]
    for b in range(1, 4):
        packed = jnp.where(lane64 == b, kv_sum[64 * b : 64 * b + 64], packed)
    prj[rep, 0:SEQ] = own_cols.astype(BF)
    prj[rep, SEQ:320] = packed.astype(BF)
    for k in range(1, REPS):
        rcopy(prj.at[rep], prj.at[rep], pr_send, pr_recv.at[rep], mate(k), grp).start()
    for k in range(1, REPS):
        s = mate(k)
        rcopy(nstage, nfull.at[:, pl.ds(pl.multiple_of(s * 32, 32), 32)], nf_send, nf_recv.at[s], s, grp).wait_recv()
    for k in range(1, REPS):
        s = mate(k)
        rcopy(prj.at[s], prj.at[s], pr_send, pr_recv.at[s], s, grp).wait_recv()

    for which in range(2):
        parts = [prj[4 * which + r, SEQ:320].astype(F32) for r in range(4)]
        for b in range(4):
            whole = jnp.zeros((64, HD), F32)
            for r in range(4):
                turned = parts[r] if r == b else pltpu.roll(parts[r], (32 * (r - b)) % 128, 1)
                whole = jnp.where(lane64 == r, turned, whole)
            kv_ref[which, 64 * b : 64 * b + 64] = whole.astype(BF)

    scale = 1.0 / jnp.sqrt(jnp.float32(HD))
    keys, vals = kv_ref[0], kv_ref[1]
    key_grad = jnp.zeros((SEQ, HD), F32)
    val_grad = jnp.zeros((SEQ, HD), F32)

    def put(cols, product):
        g32[:, :, cols] = product.reshape(PIECES, 8, HD)

    for h in range(HQ):
        q, a = prj[h, 0:SEQ], prj[HQ + h, 0:SEQ]
        scores = dot(q, keys, ((1,), (1,))) * scale
        scores = jnp.where(allow[...] > 0.5, scores, -jnp.inf)
        expon = jnp.exp(scores - jnp.max(scores, axis=1, keepdims=True))
        probs = expon / jnp.sum(expon, axis=1, keepdims=True)
        factor = 1.0 + nfull[h].astype(F32)
        dropped = (probs * factor).astype(BF)
        attended = dot(dropped, vals).astype(BF)
        val_grad = val_grad + dot(dropped, a, ((0,), (0,)))
        prob_grad = dot(a, vals, ((1,), (1,))) * factor
        inner = jnp.sum(probs * prob_grad, axis=1, keepdims=True)
        score_grad = (probs * (prob_grad - inner) * scale).astype(BF)
        query_grad = dot(score_grad, keys).astype(BF)
        key_grad = key_grad + dot(score_grad, q, ((0,), (0,)))
        put(slice(128 * h, 128 * h + 128), dot(xo_t[...], query_grad))
        put(slice(768 + 128 * h, 896 + 128 * h), dot(yo_t[...], attended))
    put(slice(512, 640), dot(xo_t[...], key_grad.astype(BF)))
    put(slice(640, 768), dot(xo_t[...], val_grad.astype(BF)))

    theirs, mine = (1 - core) * 32, core * 32
    for i in range(2):
        xs = (1 - x_lo) if i == 0 else x_lo
        gs[i] = g32[pl.ds(theirs + xs * 16, 16)].astype(BF)
        rcopy(gs.at[i], r1.at[i], r1_send, r1_recv.at[i], rep, partner).start()

    order = [2 * REACH] + [d for s in range(2 * REACH - 1, 0, -1) for d in (s, -s)] + [0]
    rcopy(gs.at[0], r1.at[0], r1_send, r1_recv.at[0], rep, partner).wait_recv()
    s2[...] = (g32[pl.ds(mine + (1 - x_lo) * 16, 16)] + r1[0].astype(F32)).astype(BF)

    def cross(zz):
        return rcopy(s2.at[zz], r2.at[zz], r2_send, r2_recv.at[zz], rep, beside)

    for d in order:
        cross(along(d)).start()
    rcopy(gs.at[1], r1.at[1], r1_send, r1_recv.at[1], rep, partner).wait_recv()
    acc[...] = g32[pl.ds(mine + x_lo * 16, 16)] + r1[1].astype(F32)

    def hop(zz, dst, rsem, d):
        return rcopy(s3.at[zz], dst, r3_send, rsem, rep, at_z(along(d)))

    def fin_copy(zz, d):
        i = d + REACH if d < 0 else d + REACH - 1
        return hop(zz, fin.at[i], fin_recv.at[i], d)

    def relay_copy(zz, d):
        i = d + REACH - 1 if d < 0 else d + REACH - 2
        return hop(zz, relay.at[i], relay_recv.at[i], d)

    for d in order:
        zz = along(d)
        cross(zz).wait_recv()
        total = acc[zz] + r2[zz].astype(F32)
        if d == 0 or abs(d) == REACH:
            acc[zz] = total
            continue
        s3[zz] = total.astype(BF)
        if abs(d) > REACH:
            relay_copy(zz, d - REACH if d > 0 else d + REACH).start()
        else:
            fin_copy(zz, d).start()
    for sign in (1, -1):
        zz = along(sign * REACH)
        total = acc[zz]
        for s in range(REACH if sign > 0 else REACH - 1, 0, -1):
            d = sign * s
            i = d + REACH - 1 if d < 0 else d + REACH - 2
            relay_copy(zz, d).wait_recv()
            total = total + relay[i].astype(F32)
        s3[zz] = total.astype(BF)
        fin_copy(zz, sign * REACH).start()
    total = acc[z]
    for s in range(1, REACH + 1):
        for d in (s, -s):
            i = d + REACH if d < 0 else d + REACH - 1
            fin_copy(z, d).wait_recv()
            total = total + fin[i].astype(F32)
    out_ref[...] = total[0:ROWS]

    def sent(ref, sem):
        pltpu.make_async_copy(ref, ref, sem).wait()

    sent(p0s.at[pl.ds(0, 7)], p0_send)
    sent(nrecv.at[pl.ds(0, 7)], nz_send)
    for k in range(1, REPS):
        rcopy(nstage, nfull.at[:, rows_own], nf_send, nf_recv.at[rep], mate(k), grp).wait_send()
    sent(wbuf.at[:, pl.ds(0, 63)], w_send)
    sent(prj.at[pl.ds(0, 7)], pr_send)
    sent(gs, r1_send)
    sent(s2, r2_send)
    sent(s3.at[pl.ds(0, 15)], r3_send)


def per_device(x, y, wqkv, wo, lab, noise, filt):
    vm = pltpu.VMEM
    dma = pltpu.SemaphoreType.DMA
    vspec = pl.BlockSpec(memory_space=pltpu.VMEM)
    anys = pl.BlockSpec(memory_space=pl.ANY)
    return pl.pallas_call(
        kernel,
        out_shape=jax.ShapeDtypeStruct((ROWS, OUTC), F32),
        in_specs=[anys, anys, vspec, vspec, vspec, anys, pl.BlockSpec(memory_space=pltpu.SMEM)],
        out_specs=vspec,
        scratch_shapes=[
            vm((SEQ, D), BF),
            vm((SEQ, D), BF),
            vm((SEQ, 512), BF),
            vm((896, 1024), BF),
            vm((512, 512), BF),
            vm((4, SEQ, 1024), BF),
            vm((4, SEQ, 1024), BF),
            vm((512, SEQ), BF),
            vm((512, SEQ), BF),
            vm((REPS, 2, 8, 128), BF),
            vm((REPS, 2, 8, 128), BF),
            vm((5, PIECES, 16, 128), BF),
            vm((REPS, 32, HQ, SEQ), BF),
            vm((HQ, 32, SEQ), BF),
            vm((HQ, SEQ, SEQ), BF),
            vm((REPS, 320, HD), BF),
            vm((2, SEQ, HD), BF),
            vm((PIECES, 8, OUTC), F32),
            vm((2, NZ, 8, OUTC), BF),
            vm((2, NZ, 8, OUTC), BF),
            vm((NZ, 8, OUTC), BF),
            vm((NZ, 8, OUTC), BF),
            vm((NZ, 8, OUTC), F32),
            vm((NZ, 8, OUTC), BF),
            vm((2 * REACH - 1, 8, OUTC), BF),
            vm((2 * REACH, 8, OUTC), BF),
            vm((SEQ, SEQ), F32),
            dma((4,)),
            dma, dma((REPS,)),
            dma, dma((REPS,)),
            dma, dma((REPS,)),
            dma, dma((PIECES,)),
            dma, dma((REPS,)),
            dma, dma((2,)),
            dma, dma((NZ,)),
            dma, dma((2 * REACH - 1,)), dma((2 * REACH,)),
        ],
        compiler_params=pltpu.CompilerParams(
            collective_id=0, has_side_effects=True, vmem_limit_bytes=56 * 1024 * 1024
        ),
    )(x, y, wqkv, wo, lab, noise, filt.reshape(1, REPS))


def solution(mesh):
    return jax.shard_map(
        per_device,
        mesh=mesh,
        in_specs=(
            P("grp", None),
            P("grp", None),
            P(("rep", "grp"), None),
            P(("rep", "grp"), None),
            P("grp", None),
            P("rep", "grp", None, None),
            P(None, "grp"),
        ),
        out_specs=P(("rep", "grp"), None),
        check_vma=False,
    )
```

time: 332 us -> 73.9 us (0.22); the launches traced: 327 us -> 73.6 us
  blocking collectives: 150 us -> 0 us
  waiting for transfers between devices: 125 us -> 0 us
  Pallas kernels: 0 us -> 72.2 us
  matrix products: 19.5 us -> 0 us
  between operations: 15.7 us -> 0.01 us
  local copies, waits for them, and re-layouts: 11.5 us -> 1.4 us
  other arithmetic: 4.81 us -> 0 us
    psum x1 -> x0, blocking collectives: 78.7 us -> none  [in_one(): total = lax.psum(jnp.concatenate([a.ravel() for a in arrays]), axis)]
    pallas_call x0 -> x1, Pallas kernels: none -> 72.2 us  [per_device(): pl.pallas_call(kernel, out_shape=jax.ShapeDtypeStruct((ROWS, OUTC), F32),...]
    all_to_all x1 -> x0, blocking collectives: 71.8 us -> none  [sent_and_summed(): lax.all_to_all(cut_along(value, dim, devices), axis, 0, 0, tiled=True)]
    all_gather x1 -> x0, waiting for transfers between devices: 71.5 us -> none  [in_one_piece(): lax.all_gather(both, axis, axis=dim, tiled=True)]
    psum x2 -> x0, waiting for transfers between devices: 53.3 us -> none  [from_root(): value = lax.psum(value, axis)]
    dot_general x9 -> x0, matrix products: 18.1 us -> none  [the longest x1 3.38 us: token_grads(): jnp.einsum('hij,jd->ihd', score_wide, keys_wide).astype(jnp.bfloat16)]
  transfers between devices with their start and end apart: 3 -> 0, of which waited for: 2 -> 0; matrix products, arithmetic and copies ran while one was open for 4% -> 0% of each run, Pallas kernels for 0% -> 0%
where the time goes in v1:
time: 73.9 us; the launch traced here: 73.6 us
  Pallas kernels  72.2 us (98%)
  local copies, waits for them, and re-layouts  1.4 us (2%)
    pallas_call x1, Pallas kernels, per_device(): pl.pallas_call(kernel, out_shape=jax.ShapeDtypeStruct((ROWS, OUTC), F32),...  72.2 us

profile of v1, /device:TPU:24, one launch (start us, length us, event | category | flops | bytes accessed | tf_op | source)
XLA Modules:
  0.0 73.6 jit_solution(3539611400050340647)
XLA Ops:
  0.0 72.2 %shard_map.73 = f32[7,1280]{1,0:T(8,128)} custom-call(bf16[256,3584]{1,0:T(8,128)(2,1)} %x_hbm.1, bf16[256,3584]{1,0:T(8,128)(2,1)} %y_hbm.1, bf16[7,768]{1,0:T(8,128)(2,1)} %wqkv_ref.1, bf16[7,512]{1,0:T(8,128)(2,1)} %wo_ref.1, s32[1,256]{1,0:T(1,128)} %lab_ref.1, bf16[1,256,4,256]{3,2,1,0:T(4,128)(2,1)} %noise_hbm.1, s32[1,8]{1,0:T(1,128)} %bitcast.1), custom_call_target="tpu_custom_call" | custom-call | tf_op jit(solution)/shard_map/pallas_call | solution.py:385
  72.2 1.4 %copy.9 = f32[7,1280]{1,0:T(8,128)} copy(f32[7,1280]{1,0:T(8,128)} %shard_map.73) | data formatting | bytes 71680

commit v2 on v1

v2 whole, which is shorter than its diff:
```python
import functools

import jax
import jax.numpy as jnp
from jax import lax
from jax.experimental import pallas as pl
from jax.experimental.pallas import tpu as pltpu
from jax.sharding import PartitionSpec as P

MESH = pl.DeviceIdType.MESH
BF = jnp.bfloat16
F32 = jnp.float32
REPS = 8
NZ = 16
PIECES = 64
REACH = 4
SEQ = 256
D = 3584
HD = 128
HQ = 4
ROWS = 7
OUTC = 1280


def iota(shape, dim):
    return lax.broadcasted_iota(jnp.int32, shape, dim)


def dot(a, b, dims=((1,), (0,))):
    return lax.dot_general(a, b, (dims, ((), ())), preferred_element_type=F32)


def kernel(
    x_hbm, y_hbm, wqkv_ref, wo_ref, lab_ref, noise_hbm, filt_ref,
    out_ref,
    xb, zb, yw, sel_e, own_e, xe, ze, xo_t, yo_t, p0s, p0r, wbuf,
    nhi, nband, nrecv, nstage, nfull, prj, kvp, kv_ref, allow,
    ga, gsa, r1a, s2a, r2a, acca, s3a, relaya, fina,
    gb, gsb, r1b, s2b, r2b, accb, s3b, relayb, finb,
    loc, p0_send, p0_recv, nz_send, nz_recv, nf_send, nf_recv, w_send, w_recv,
    kv_send, kv_recv, pr_send, pr_recv,
    r1_send, r1_recv, r2_send, r2_recv, r3_send, relay_recv, fin_recv,
):
    rep = lax.axis_index("rep")
    grp = lax.axis_index("grp")
    x_lo = grp // 32
    z = (grp // 2) % NZ
    core = grp % 2
    partner = grp + 1 - 2 * core
    beside = grp + 32 - 64 * x_lo

    def along(d):
        return lax.rem(z + (d + NZ), NZ)

    def at_z(zz):
        return x_lo * 32 + zz * 2 + core

    def rcopy(src, dst, ssem, rsem, r, g):
        return pltpu.make_async_remote_copy(
            src_ref=src, dst_ref=dst, send_sem=ssem, recv_sem=rsem,
            device_id=(r, g), device_id_type=MESH,
        )

    def mate(k):
        return lax.rem(rep + k, REPS)

    barrier = pltpu.get_barrier_semaphore()
    near = [d for s in range(REACH, 0, -1) for d in (s, -s)]
    for k in range(1, REPS):
        pl.semaphore_signal(barrier, inc=1, device_id=(mate(k), grp), device_id_type=MESH)
    for d in near:
        pl.semaphore_signal(barrier, inc=1, device_id=(rep, at_z(along(d))), device_id_type=MESH)
    pl.semaphore_signal(barrier, inc=1, device_id=(rep, partner), device_id_type=MESH)
    pl.semaphore_signal(barrier, inc=1, device_id=(rep, beside), device_id_type=MESH)

    window = pl.multiple_of(128 * (3 * rep + rep // 2), 128)
    shift_own = 64 * (rep % 2)
    cnh = pltpu.make_async_copy(noise_hbm.at[0, pl.ds(128, 128)], nhi, loc.at[3])
    cnh.start()
    cnl = pltpu.make_async_copy(
        noise_hbm.at[0, pl.ds(0, 128), :, pl.ds(0, 128)], nband.at[pl.ds(0, 128)], loc.at[4]
    )
    cnl.start()
    cx = pltpu.make_async_copy(x_hbm, xb, loc.at[0])
    cx.start()
    czx = pltpu.make_async_copy(x_hbm, zb, loc.at[1])
    czy = pltpu.make_async_copy(y_hbm, zb, loc.at[1])

    @pl.when(rep < HQ)
    def _():
        czx.start()

    @pl.when(rep >= HQ)
    def _():
        czy.start()

    cy = pltpu.make_async_copy(y_hbm.at[:, pl.ds(window, 512)], yw, loc.at[2])
    cy.start()

    zero_row = jnp.zeros((1, 768), F32)
    wq = jnp.concatenate([wqkv_ref[...].astype(F32), zero_row], axis=0)
    wo = jnp.concatenate([wo_ref[...].astype(F32), zero_row[:, :512]], axis=0)
    lane8 = iota((8, 128), 1)
    slot = rep // 2
    for d in range(REPS):
        if d < HQ:
            chunk, kv = wq[:, 128 * d : 128 * d + 128], wq[:, 512:640]
        else:
            chunk, kv = wo[:, 128 * (d - HQ) : 128 * (d - HQ) + 128], wq[:, 640:768]
        turned = pltpu.roll(kv, lax.rem(32 * slot + 128 - 32 * (d % 4), 128), 1)
        p0s[d, 0] = chunk.astype(BF)
        p0s[d, 1] = jnp.where(lane8 // 32 == slot, turned, 0.0).astype(BF)
    p0r[rep] = p0s[rep]

    pl.semaphore_wait(barrier, len(near) + REPS - 1 + 2)

    for k in range(1, REPS):
        rcopy(p0s.at[mate(k)], p0r.at[rep], p0_send, p0_recv.at[rep], mate(k), grp).start()

    cnh.wait()

    def band(i, carry):
        rows = pl.ds(pl.multiple_of(16 * i, 16), 16)
        low = nhi[rows, :, 0:128].astype(F32)
        high = nhi[rows, :, 128:256].astype(F32)
        keep = iota((16, HQ, 128), 2) > iota((16, HQ, 128), 0) + 16 * i
        nband[pl.ds(pl.multiple_of(128 + 16 * i, 16), 16)] = jnp.where(keep, low, high).astype(BF)
        return carry

    lax.fori_loop(0, 8, band, 0)
    cnl.wait()

    def slice_of(r):
        return nband.at[pl.ds(pl.multiple_of(r * 32, 32), 32)]

    for k in range(1, REPS):
        rcopy(slice_of(mate(k)), nrecv.at[rep], nz_send, nz_recv.at[rep], mate(k), grp).start()
    nrecv[rep] = nband[pl.ds(pl.multiple_of(rep * 32, 32), 32)]

    col = iota((128, 1024), 1)
    part = col % 16
    target = 448 * (part // 8) + 7 * (col // 16) + part % 8
    target = jnp.where(part % 8 < ROWS, target, -1)

    def fill_e(b, carry):
        sel_e[pl.ds(pl.multiple_of(128 * b, 128), 128), :] = jnp.where(
            iota((128, 1024), 0) + 128 * b == target, 1.0, 0.0
        ).astype(BF)
        return carry

    lax.fori_loop(0, 7, fill_e, 0)

    for k in range(1, REPS):
        s = mate(k)
        rcopy(p0s.at[s], p0r.at[s], p0_send, p0_recv.at[s], s, grp).wait_recv()
    for t in range(4):
        wbuf[t, grp, 0:8] = p0r[2 * t, 0]
        wbuf[t, grp, 8:16] = p0r[2 * t + 1, 0]
    for half in range(2):
        total = p0r[half, 1].astype(F32)
        for b in range(1, 4):
            total = total + p0r[2 * b + half, 1].astype(F32)
        wbuf[4, grp, 8 * half : 8 * half + 8] = total.astype(BF)

    def piece(p, g):
        return rcopy(wbuf.at[:, p], wbuf.at[:, p], w_send, w_recv.at[p], rep, g)

    for d in near:
        piece(grp, at_z(along(d))).start()
    piece(grp, beside).start()
    piece(grp, partner).start()

    cx.wait()
    czx.wait()

    def spread(t):
        lanes = pl.ds(pl.multiple_of(896 * t, 128), 896)

        xe[t] = dot(xb[:, lanes], sel_e[...]).astype(BF)
        ze[t] = dot(zb[:, lanes], sel_e[...]).astype(BF)

    def land(d):
        p = at_z(along(d))
        piece(p, grp).wait_recv()
        return p

    def hand_on(p):
        piece(p, beside).start()
        piece(p, partner).start()

    spread(0)

    p = land(-REACH)
    for s in range(REACH, 0, -1):
        piece(p, at_z(along(s))).start()
    hand_on(p)
    p = land(REACH)
    for s in range(REACH - 1, 0, -1):
        piece(p, at_z(along(-s))).start()
    hand_on(p)
    for s in range(1, REACH):
        hand_on(land(-s))
        hand_on(land(s))

    spread(1)

    for k in range(1, REPS):
        s = mate(k)
        rcopy(slice_of(s), nrecv.at[s], nz_send, nz_recv.at[s], s, grp).wait_recv()
    kept = nrecv[0].astype(F32)
    for s in range(1, REPS):
        kept = jnp.where(filt_ref[0, s] == 1, nrecv[s].astype(F32), kept)
    rows_own = pl.ds(pl.multiple_of(rep * 32, 32), 32)
    for h in range(HQ):
        rows = kept[:, h, :].astype(BF)
        nstage[h] = rows
        nfull[h, rows_own] = rows
    for k in range(1, REPS):
        rcopy(nstage, nfull.at[:, rows_own], nf_send, nf_recv.at[rep], mate(k), grp).start()

    spread(2)
    spread(3)

    for s in range(REACH + 1, 2 * REACH):
        hand_on(land(-s))
        hand_on(land(s))
    hand_on(land(-2 * REACH))

    outward = [0] + [d for s in range(1, 2 * REACH) for d in (-s, s)] + [2 * REACH]
    for d in outward:
        q = (1 - x_lo) * 32 + along(d) * 2 + core
        piece(q, grp).wait_recv()
        piece(q, partner).start()

    def from_partner(side):
        def one(i, carry):
            piece(side * 32 + lax.rem(z + i, NZ) * 2 + 1 - core, grp).wait_recv()
            return carry

        lax.fori_loop(0, NZ, one, 0)

    lane = iota((SEQ, HD), 1) // 32

    def kv_part(side):
        w = wbuf[4, pl.ds(side * 32, 32)].reshape(512, HD)
        lanes = pl.ds(pl.multiple_of(512 * side, 128), 512)
        total = jnp.zeros((SEQ, HD), F32)
        for b in range(4):
            total = jnp.where(lane == b, dot(xe[b, :, lanes], w), total)
        return total

    def own_part(side):
        lanes = pl.ds(pl.multiple_of(512 * side, 128), 512)
        total = jnp.zeros((SEQ, HD), F32)
        for t in range(4):
            total = total + dot(ze[t, :, lanes], wbuf[t, pl.ds(side * 32, 32)].reshape(512, HD))
        return total

    from_partner(x_lo)
    kv_sum = kv_part(x_lo)
    own_cols = own_part(x_lo)
    from_partner(1 - x_lo)
    kv_sum = kv_sum + kv_part(1 - x_lo)
    kv_sum = kv_sum + pltpu.roll(kv_sum, 64, 1)
    kv_sum = kv_sum + pltpu.roll(kv_sum, 32, 1)
    lane64 = iota((64, HD), 1) // 32
    packed = kv_sum[0:64]
    for b in range(1, 4):
        packed = jnp.where(lane64 == b, kv_sum[64 * b : 64 * b + 64], packed)
    kvp[rep] = packed.astype(BF)
    far_first = (2, 6, 1, 3, 5, 7, 4)
    for k in far_first:
        rcopy(kvp.at[rep], kvp.at[rep], kv_send, kv_recv.at[rep], mate(k), grp).start()
    own_cols = own_cols + own_part(1 - x_lo)
    prj[rep] = own_cols.astype(BF)
    for k in (4, 1, 3, 5, 7, 2, 6):
        rcopy(prj.at[rep], prj.at[rep], pr_send, pr_recv.at[rep], mate(k), grp).start()

    crow = iota((512, 128), 0)
    pidx = crow // 8
    owner = ((pidx // 16) % 2) * 32 + (pidx % 16) * 2 + pidx // 32
    want = shift_own + 7 * owner + crow % 8
    want = jnp.where(crow % 8 < ROWS, want, -1)
    for b in range(4):
        own_e[:, 128 * b : 128 * b + 128] = jnp.where(
            iota((512, 128), 1) + 128 * b == want, 1.0, 0.0
        ).astype(BF)
    cy.wait()
    xo_t[...] = dot(own_e[...], xb[:, pl.ds(window, 512)], ((1,), (1,))).astype(BF)
    yo_t[...] = dot(own_e[...], yw[...], ((1,), (1,))).astype(BF)

    lab = lab_ref[...]
    qi, kj = iota((SEQ, SEQ), 0), iota((SEQ, SEQ), 1)
    lab_col = jnp.sum(jnp.where(qi == kj, lab, 0), axis=1, keepdims=True)
    allow[...] = jnp.where((lab_col == lab) & (kj <= qi), 1.0, 0.0)

    for k in range(1, REPS):
        s = mate(k)
        rcopy(kvp.at[s], kvp.at[s], kv_send, kv_recv.at[s], s, grp).wait_recv()
    for which in range(2):
        parts = [kvp[4 * which + r].astype(F32) for r in range(4)]
        for b in range(4):
            whole = jnp.zeros((64, HD), F32)
            for r in range(4):
                turned = parts[r] if r == b else pltpu.roll(parts[r], (32 * (r - b)) % 128, 1)
                whole = jnp.where(lane64 == r, turned, whole)
            kv_ref[which, 64 * b : 64 * b + 64] = whole.astype(BF)
    for k in range(1, REPS):
        s = mate(k)
        rcopy(nstage, nfull.at[:, pl.ds(pl.multiple_of(s * 32, 32), 32)], nf_send, nf_recv.at[s], s, grp).wait_recv()

    scale = 1.0 / jnp.sqrt(jnp.float32(HD))
    keys, vals = kv_ref[0], kv_ref[1]
    key_grad = jnp.zeros((SEQ, HD), F32)
    val_grad = jnp.zeros((SEQ, HD), F32)

    def put(g32, at, product):
        g32[:, :, 128 * at : 128 * at + 128] = product.reshape(PIECES, 8, HD)

    heads = [lax.rem(rep + o, HQ) for o in (0, 1, 3, 2)]

    def attend(i, key_grad, val_grad):
        h = heads[i]
        if i == 0:
            s = mate(HQ)
            rcopy(prj.at[s], prj.at[s], pr_send, pr_recv.at[s], s, grp).wait_recv()
        else:
            for s in (h, HQ + h):
                rcopy(prj.at[s], prj.at[s], pr_send, pr_recv.at[s], s, grp).wait_recv()
        q, a = prj[h], prj[HQ + h]
        scores = dot(q, keys, ((1,), (1,))) * scale
        scores = jnp.where(allow[...] > 0.5, scores, -jnp.inf)
        expon = jnp.exp(scores - jnp.max(scores, axis=1, keepdims=True))
        probs = expon / jnp.sum(expon, axis=1, keepdims=True)
        factor = 1.0 + nfull[h].astype(F32)
        factor = jnp.concatenate([factor, factor], axis=1)
        dropped = (probs * factor).astype(BF)
        attended = dot(dropped, vals).astype(BF)
        val_grad = val_grad + dot(dropped, a, ((0,), (0,)))
        prob_grad = dot(a, vals, ((1,), (1,))) * factor
        inner = jnp.sum(probs * prob_grad, axis=1, keepdims=True)
        score_grad = (probs * (prob_grad - inner) * scale).astype(BF)
        query_grad = dot(score_grad, keys).astype(BF)
        key_grad = key_grad + dot(score_grad, q, ((0,), (0,)))
        g32 = ga if i < 2 else gb
        put(g32, 2 * (i % 2), dot(xo_t[...], query_grad))
        put(g32, 2 * (i % 2) + 1, dot(yo_t[...], attended))
        return key_grad, val_grad

    theirs, mine = (1 - core) * 32, core * 32
    order = [2 * REACH] + [d for s in range(2 * REACH - 1, 0, -1) for d in (s, -s)] + [0]

    def relay_at(d):
        return d + REACH - 1 if d < 0 else d + REACH - 2

    def fin_at(d):
        return d + REACH if d < 0 else d + REACH - 1

    class Sums:
        def __init__(self, n, g32, gs, r1, s2, r2, acc, s3, relay, fin):
            self.n, self.g32, self.gs, self.r1, self.s2, self.r2 = n, g32, gs, r1, s2, r2
            self.acc, self.s3, self.relay, self.fin = acc, s3, relay, fin

        def core_copy(self, i):
            return rcopy(self.gs.at[i], self.r1.at[i], r1_send.at[self.n], r1_recv.at[self.n, i], rep, partner)

        def cross(self, zz):
            return rcopy(self.s2.at[zz], self.r2.at[zz], r2_send.at[self.n], r2_recv.at[self.n, zz], rep, beside)

        def hop(self, zz, dst, rsem, d):
            return rcopy(self.s3.at[zz], dst, r3_send.at[self.n], rsem, rep, at_z(along(d)))

        def fin_copy(self, zz, d):
            return self.hop(zz, self.fin.at[fin_at(d)], fin_recv.at[self.n, fin_at(d)], d)

        def relay_copy(self, zz, d):
            return self.hop(zz, self.relay.at[relay_at(d)], relay_recv.at[self.n, relay_at(d)], d)

        def to_partner(self):
            for i in range(2):
                xs = (1 - x_lo) if i == 0 else x_lo
                self.gs[i] = self.g32[pl.ds(theirs + xs * 16, 16)].astype(BF)
                self.core_copy(i).start()

        def to_beside(self):
            self.core_copy(0).wait_recv()
            self.s2[...] = (
                self.g32[pl.ds(mine + (1 - x_lo) * 16, 16)] + self.r1[0].astype(F32)
            ).astype(BF)
            for d in order:
                self.cross(along(d)).start()
            self.core_copy(1).wait_recv()
            self.acc[...] = self.g32[pl.ds(mine + x_lo * 16, 16)] + self.r1[1].astype(F32)

        def to_z(self):
            for d in order:
                zz = along(d)
                self.cross(zz).wait_recv()
                total = self.acc[zz] + self.r2[zz].astype(F32)
                if d == 0 or abs(d) == REACH:
                    self.acc[zz] = total
                    continue
                self.s3[zz] = total.astype(BF)
                if abs(d) > REACH:
                    self.relay_copy(zz, d - REACH if d > 0 else d + REACH).start()
                else:
                    self.fin_copy(zz, d).start()

        def relays(self):
            for sign in (1, -1):
                zz = along(sign * REACH)
                total = self.acc[zz]
                for s in range(REACH if sign > 0 else REACH - 1, 0, -1):
                    self.relay_copy(zz, sign * s).wait_recv()
                    total = total + self.relay[relay_at(sign * s)].astype(F32)
                self.s3[zz] = total.astype(BF)
                self.fin_copy(zz, sign * REACH).start()

        def final(self):
            total = self.acc[z]
            for s in range(1, REACH + 1):
                for d in (s, -s):
                    self.fin_copy(z, d).wait_recv()
                    total = total + self.fin[fin_at(d)].astype(F32)
            return total

    first = Sums(0, ga, gsa, r1a, s2a, r2a, acca, s3a, relaya, fina)
    last = Sums(1, gb, gsb, r1b, s2b, r2b, accb, s3b, relayb, finb)

    key_grad, val_grad = attend(0, key_grad, val_grad)
    key_grad, val_grad = attend(1, key_grad, val_grad)
    first.to_partner()
    key_grad, val_grad = attend(2, key_grad, val_grad)
    first.to_beside()
    key_grad, val_grad = attend(3, key_grad, val_grad)
    put(gb, 4, dot(xo_t[...], key_grad.astype(BF)))
    put(gb, 5, dot(xo_t[...], val_grad.astype(BF)))
    last.to_partner()
    last.to_beside()
    first.to_z()
    first.relays()
    last.to_z()
    last.relays()

    def write(total, at, lanes):
        out_ref[:, lanes] = total[0:ROWS, 128 * at : 128 * at + 128]

    for group, total in ((0, first.final()), (1, last.final())):
        for i in range(2):
            h = heads[2 * group + i]
            write(total, 2 * i, pl.ds(pl.multiple_of(128 * h, 128), 128))
            write(total, 2 * i + 1, pl.ds(pl.multiple_of(768 + 128 * h, 128), 128))
        if group == 1:
            write(total, 4, pl.ds(512, 128))
            write(total, 5, pl.ds(640, 128))

    def sent(ref, sem):
        pltpu.make_async_copy(ref, ref, sem).wait()

    sent(p0s.at[pl.ds(0, 7)], p0_send)
    sent(nrecv.at[pl.ds(0, 7)], nz_send)
    for k in range(1, REPS):
        rcopy(nstage, nfull.at[:, rows_own], nf_send, nf_recv.at[rep], mate(k), grp).wait_send()
    sent(wbuf.at[:, pl.ds(0, 63)], w_send)
    sent(kvp.at[pl.ds(0, 7)], kv_send)
    sent(prj.at[pl.ds(0, 7)], pr_send)
    for g in (first, last):
        sent(g.gs, r1_send.at[g.n])
        sent(g.s2, r2_send.at[g.n])
        sent(g.s3.at[pl.ds(0, 15)], r3_send.at[g.n])


def per_device(x, y, wqkv, wo, lab, noise, filt):
    vm = pltpu.VMEM
    dma = pltpu.SemaphoreType.DMA
    vspec = pl.BlockSpec(memory_space=pltpu.VMEM)
    anys = pl.BlockSpec(memory_space=pl.ANY)
    return pl.pallas_call(
        kernel,
        out_shape=jax.ShapeDtypeStruct((ROWS, OUTC), F32),
        in_specs=[anys, anys, vspec, vspec, vspec, anys, pl.BlockSpec(memory_space=pltpu.SMEM)],
        out_specs=vspec,
        scratch_shapes=[
            vm((SEQ, D), BF),
            vm((SEQ, D), BF),
            vm((SEQ, 512), BF),
            vm((896, 1024), BF),
            vm((512, 512), BF),
            vm((4, SEQ, 1024), BF),
            vm((4, SEQ, 1024), BF),
            vm((512, SEQ), BF),
            vm((512, SEQ), BF),
            vm((REPS, 2, 8, 128), BF),
            vm((REPS, 2, 8, 128), BF),
            vm((5, PIECES, 16, 128), BF),
            vm((128, HQ, SEQ), BF),
            vm((SEQ, HQ, 128), BF),
            vm((REPS, 32, HQ, 128), BF),
            vm((HQ, 32, 128), BF),
            vm((HQ, SEQ, 128), BF),
            vm((REPS, SEQ, HD), BF),
            vm((REPS, 64, HD), BF),
            vm((2, SEQ, HD), BF),
            vm((SEQ, SEQ), F32),
        ]
        + [
            s
            for width in (512, 768)
            for s in (
                vm((PIECES, 8, width), F32),
                vm((2, NZ, 8, width), BF),
                vm((2, NZ, 8, width), BF),
                vm((NZ, 8, width), BF),
                vm((NZ, 8, width), BF),
                vm((NZ, 8, width), F32),
                vm((NZ, 8, width), BF),
                vm((2 * REACH - 1, 8, width), BF),
                vm((2 * REACH, 8, width), BF),
            )
        ]
        + [
            dma((5,)),
            dma, dma((REPS,)),
            dma, dma((REPS,)),
            dma, dma((REPS,)),
            dma, dma((PIECES,)),
            dma, dma((REPS,)),
            dma, dma((REPS,)),
            dma((2,)), dma((2, 2)),
            dma((2,)), dma((2, NZ)),
            dma((2,)), dma((2, 2 * REACH - 1)), dma((2, 2 * REACH)),
        ],
        compiler_params=pltpu.CompilerParams(
            collective_id=0, has_side_effects=True, vmem_limit_bytes=56 * 1024 * 1024
        ),
    )(x, y, wqkv, wo, lab, noise, filt.reshape(1, REPS))


def solution(mesh):
    return jax.shard_map(
        per_device,
        mesh=mesh,
        in_specs=(
            P("grp", None),
            P("grp", None),
            P(("rep", "grp"), None),
            P(("rep", "grp"), None),
            P("grp", None),
            P("rep", "grp", None, None),
            P(None, "grp"),
        ),
        out_specs=P(("rep", "grp"), None),
        check_vma=False,
    )
```

time: 73.9 us -> 70.1 us (0.949)
  Pallas kernels: 72.2 us -> 68.1 us
    pallas_call x1, Pallas kernels: 72.2 us -> 68.1 us  [per_device(): pl.pallas_call(kernel, out_shape=jax.ShapeDtypeStruct((ROWS, OUTC), F32),...]
where the time goes in v2:
time: 70.1 us; the launch traced here: 69.5 us
  Pallas kernels  68.1 us (97%)
  local copies, waits for them, and re-layouts  1.4 us (2%)
    pallas_call x1, Pallas kernels, per_device(): pl.pallas_call(kernel, out_shape=jax.ShapeDtypeStruct((ROWS, OUTC), F32),...  68.1 us

profile of v2, /device:TPU:24, one launch (start us, length us, event | category | flops | bytes accessed | tf_op | source)
XLA Modules:
  0.0 69.5 jit_solution(6929030392444485244)
XLA Ops:
  0.0 68.1 %shard_map.73 = f32[7,1280]{1,0:T(8,128)} custom-call(bf16[256,3584]{1,0:T(8,128)(2,1)} %x_hbm.1, bf16[256,3584]{1,0:T(8,128)(2,1)} %y_hbm.1, bf16[7,768]{1,0:T(8,128)(2,1)} %wqkv_ref.1, bf16[7,512]{1,0:T(8,128)(2,1)} %wo_ref.1, s32[1,256]{1,0:T(1,128)} %lab_ref.1, bf16[1,256,4,256]{3,2,1,0:T(4,128)(2,1)} %noise_hbm.1, s32[1,8]{1,0:T(1,128)} %bitcast.1), custom_call_target="tpu_custom_call" | custom-call | tf_op jit(solution)/shard_map/pallas_call | solution.py:478
  68.1 1.4 %copy.9 = f32[7,1280]{1,0:T(8,128)} copy(f32[7,1280]{1,0:T(8,128)} %shard_map.73) | data formatting | bytes 71680

commit v3 on v2

--- a/solution.py
+++ b/solution.py
@@ -31,12 +31,13 @@
 
 
 def kernel(
-    x_hbm, y_hbm, wqkv_ref, wo_ref, lab_ref, noise_hbm, filt_ref,
-    out_ref,
+    x_hbm, y_hbm, wqkv_hbm, wo_hbm, lab_hbm, noise_hbm, filt_hbm,
+    out_ref, wqkv_ref, wo_ref, lab_ref, filt_ref,
     xb, zb, yw, sel_e, own_e, xe, ze, xo_t, yo_t, p0s, p0r, wbuf,
     nhi, nband, nrecv, nstage, nfull, prj, kvp, kv_ref, allow,
-    ga, gsa, r1a, s2a, r2a, acca, s3a, relaya, fina,
-    gb, gsb, r1b, s2b, r2b, accb, s3b, relayb, finb,
+    g_0, gs_0, r1_0, s2_0, r2_0, acc_0, s3_0, relay_0, fin_0,
+    g_1, gs_1, r1_1, s2_1, r2_1, acc_1, s3_1, relay_1, fin_1,
+    g_2, gs_2, r1_2, s2_2, r2_2, acc_2, s3_2, relay_2, fin_2,
     loc, p0_send, p0_recv, nz_send, nz_recv, nf_send, nf_recv, w_send, w_recv,
     kv_send, kv_recv, pr_send, pr_recv,
     r1_send, r1_recv, r2_send, r2_recv, r3_send, relay_recv, fin_recv,
@@ -73,6 +74,14 @@
     pl.semaphore_signal(barrier, inc=1, device_id=(rep, partner), device_id_type=MESH)
     pl.semaphore_signal(barrier, inc=1, device_id=(rep, beside), device_id_type=MESH)
 
+    small = [
+        pltpu.make_async_copy(src, dst, loc.at[5 + i])
+        for i, (src, dst) in enumerate(
+            ((wqkv_hbm, wqkv_ref), (wo_hbm, wo_ref), (lab_hbm, lab_ref), (filt_hbm, filt_ref))
+        )
+    ]
+    for c in small:
+        c.start()
     window = pl.multiple_of(128 * (3 * rep + rep // 2), 128)
     shift_own = 64 * (rep % 2)
     cnh = pltpu.make_async_copy(noise_hbm.at[0, pl.ds(128, 128)], nhi, loc.at[3])
@@ -97,6 +106,8 @@
     cy = pltpu.make_async_copy(y_hbm.at[:, pl.ds(window, 512)], yw, loc.at[2])
     cy.start()
 
+    small[0].wait()
+    small[1].wait()
     zero_row = jnp.zeros((1, 768), F32)
     wq = jnp.concatenate([wqkv_ref[...].astype(F32), zero_row], axis=0)
     wo = jnp.concatenate([wo_ref[...].astype(F32), zero_row[:, :512]], axis=0)
@@ -137,18 +148,17 @@
         rcopy(slice_of(mate(k)), nrecv.at[rep], nz_send, nz_recv.at[rep], mate(k), grp).start()
     nrecv[rep] = nband[pl.ds(pl.multiple_of(rep * 32, 32), 32)]
 
-    col = iota((128, 1024), 1)
+    low, high = (0, 0, 128, 256), (384, 512, 640, 640)
+    col = iota((256, 256), 1)
+    feature = iota((256, 256), 0)
     part = col % 16
-    target = 448 * (part // 8) + 7 * (col // 16) + part % 8
-    target = jnp.where(part % 8 < ROWS, target, -1)
-
-    def fill_e(b, carry):
-        sel_e[pl.ds(pl.multiple_of(128 * b, 128), 128), :] = jnp.where(
-            iota((128, 1024), 0) + 128 * b == target, 1.0, 0.0
+    for b in range(4):
+        want = 7 * (16 * b + col // 16) + part % 8
+        inside = part % 8 < ROWS
+        sel_e[b, 0:256] = jnp.where(inside & (part < 8) & (feature + low[b] == want), 1.0, 0.0).astype(BF)
+        sel_e[b, 256:512] = jnp.where(
+            inside & (part >= 8) & (feature + high[b] == want + 448), 1.0, 0.0
         ).astype(BF)
-        return carry
-
-    lax.fori_loop(0, 7, fill_e, 0)
 
     for k in range(1, REPS):
         s = mate(k)
@@ -174,10 +184,12 @@
     czx.wait()
 
     def spread(t):
-        lanes = pl.ds(pl.multiple_of(896 * t, 128), 896)
-
-        xe[t] = dot(xb[:, lanes], sel_e[...]).astype(BF)
-        ze[t] = dot(zb[:, lanes], sel_e[...]).astype(BF)
+        for b in range(4):
+            cols = slice(256 * b, 256 * b + 256)
+            for src, dst in ((xb, xe), (zb, ze)):
+                lo = dot(src[:, 896 * t + low[b] : 896 * t + low[b] + 256], sel_e[b, 0:256])
+                hi = dot(src[:, 896 * t + high[b] : 896 * t + high[b] + 256], sel_e[b, 256:512])
+                dst[t, :, cols] = (lo + hi).astype(BF)
 
     def land(d):
         p = at_z(along(d))
@@ -207,6 +219,7 @@
     for k in range(1, REPS):
         s = mate(k)
         rcopy(slice_of(s), nrecv.at[s], nz_send, nz_recv.at[s], s, grp).wait_recv()
+    small[3].wait()
     kept = nrecv[0].astype(F32)
     for s in range(1, REPS):
         kept = jnp.where(filt_ref[0, s] == 1, nrecv[s].astype(F32), kept)
@@ -289,6 +302,7 @@
     xo_t[...] = dot(own_e[...], xb[:, pl.ds(window, 512)], ((1,), (1,))).astype(BF)
     yo_t[...] = dot(own_e[...], yw[...], ((1,), (1,))).astype(BF)
 
+    small[2].wait()
     lab = lab_ref[...]
     qi, kj = iota((SEQ, SEQ), 0), iota((SEQ, SEQ), 1)
     lab_col = jnp.sum(jnp.where(qi == kj, lab, 0), axis=1, keepdims=True)
@@ -318,6 +332,8 @@
         g32[:, :, 128 * at : 128 * at + 128] = product.reshape(PIECES, 8, HD)
 
     heads = [lax.rem(rep + o, HQ) for o in (0, 1, 3, 2)]
+
+    place = ((g_0, 0), (g_1, 0), (g_1, 2), (g_2, 0))
 
     def attend(i, key_grad, val_grad):
         h = heads[i]
@@ -342,9 +358,9 @@
         score_grad = (probs * (prob_grad - inner) * scale).astype(BF)
         query_grad = dot(score_grad, keys).astype(BF)
         key_grad = key_grad + dot(score_grad, q, ((0,), (0,)))
-        g32 = ga if i < 2 else gb
-        put(g32, 2 * (i % 2), dot(xo_t[...], query_grad))
-        put(g32, 2 * (i % 2) + 1, dot(yo_t[...], attended))
+        g32, at = place[i]
+        put(g32, at, dot(xo_t[...], query_grad))
+        put(g32, at + 1, dot(yo_t[...], attended))
         return key_grad, val_grad
 
     theirs, mine = (1 - core) * 32, core * 32
@@ -424,35 +440,38 @@
                     total = total + self.fin[fin_at(d)].astype(F32)
             return total
 
-    first = Sums(0, ga, gsa, r1a, s2a, r2a, acca, s3a, relaya, fina)
-    last = Sums(1, gb, gsb, r1b, s2b, r2b, accb, s3b, relayb, finb)
+    one = Sums(0, g_0, gs_0, r1_0, s2_0, r2_0, acc_0, s3_0, relay_0, fin_0)
+    two = Sums(1, g_1, gs_1, r1_1, s2_1, r2_1, acc_1, s3_1, relay_1, fin_1)
+    three = Sums(2, g_2, gs_2, r1_2, s2_2, r2_2, acc_2, s3_2, relay_2, fin_2)
 
     key_grad, val_grad = attend(0, key_grad, val_grad)
+    one.to_partner()
     key_grad, val_grad = attend(1, key_grad, val_grad)
-    first.to_partner()
+    one.to_beside()
     key_grad, val_grad = attend(2, key_grad, val_grad)
-    first.to_beside()
+    two.to_partner()
+    one.to_z()
+    two.to_beside()
     key_grad, val_grad = attend(3, key_grad, val_grad)
-    put(gb, 4, dot(xo_t[...], key_grad.astype(BF)))
-    put(gb, 5, dot(xo_t[...], val_grad.astype(BF)))
-    last.to_partner()
-    last.to_beside()
-    first.to_z()
-    first.relays()
-    last.to_z()
-    last.relays()
+    put(g_2, 2, dot(xo_t[...], key_grad.astype(BF)))
+    put(g_2, 3, dot(xo_t[...], val_grad.astype(BF)))
+    three.to_partner()
+    two.to_z()
+    three.to_beside()
+    one.relays()
+    three.to_z()
+    two.relays()
+    three.relays()
 
     def write(total, at, lanes):
         out_ref[:, lanes] = total[0:ROWS, 128 * at : 128 * at + 128]
 
-    for group, total in ((0, first.final()), (1, last.final())):
-        for i in range(2):
-            h = heads[2 * group + i]
-            write(total, 2 * i, pl.ds(pl.multiple_of(128 * h, 128), 128))
-            write(total, 2 * i + 1, pl.ds(pl.multiple_of(768 + 128 * h, 128), 128))
-        if group == 1:
-            write(total, 4, pl.ds(512, 128))
-            write(total, 5, pl.ds(640, 128))
+    finals = {id(g.g32): g.final() for g in (one, two, three)}
+    for i, (g32, at) in enumerate(place):
+        write(finals[id(g32)], at, pl.ds(pl.multiple_of(128 * heads[i], 128), 128))
+        write(finals[id(g32)], at + 1, pl.ds(pl.multiple_of(768 + 128 * heads[i], 128), 128))
+    write(finals[id(g_2)], 2, pl.ds(512, 128))
+    write(finals[id(g_2)], 3, pl.ds(640, 128))
 
     def sent(ref, sem):
         pltpu.make_async_copy(ref, ref, sem).wait()
@@ -464,7 +483,7 @@
     sent(wbuf.at[:, pl.ds(0, 63)], w_send)
     sent(kvp.at[pl.ds(0, 7)], kv_send)
     sent(prj.at[pl.ds(0, 7)], pr_send)
-    for g in (first, last):
+    for g in (one, two, three):
         sent(g.gs, r1_send.at[g.n])
         sent(g.s2, r2_send.at[g.n])
         sent(g.s3.at[pl.ds(0, 15)], r3_send.at[g.n])
@@ -477,14 +496,18 @@
     anys = pl.BlockSpec(memory_space=pl.ANY)
     return pl.pallas_call(
         kernel,
-        out_shape=jax.ShapeDtypeStruct((ROWS, OUTC), F32),
-        in_specs=[anys, anys, vspec, vspec, vspec, anys, pl.BlockSpec(memory_space=pltpu.SMEM)],
+        out_shape=pltpu.VMEM((ROWS, OUTC), F32),
+        in_specs=[anys] * 7,
         out_specs=vspec,
         scratch_shapes=[
+            vm((ROWS, 768), BF),
+            vm((ROWS, 512), BF),
+            vm((1, SEQ), jnp.int32),
+            pltpu.SMEM((1, REPS), jnp.int32),
             vm((SEQ, D), BF),
             vm((SEQ, D), BF),
             vm((SEQ, 512), BF),
-            vm((896, 1024), BF),
+            vm((4, 512, 256), BF),
             vm((512, 512), BF),
             vm((4, SEQ, 1024), BF),
             vm((4, SEQ, 1024), BF),
@@ -505,7 +528,7 @@
         ]
         + [
             s
-            for width in (512, 768)
+            for width in (256, 512, 512)
             for s in (
                 vm((PIECES, 8, width), F32),
                 vm((2, NZ, 8, width), BF),
@@ -519,16 +542,16 @@
             )
         ]
         + [
-            dma((5,)),
+            dma((9,)),
             dma, dma((REPS,)),
             dma, dma((REPS,)),
             dma, dma((REPS,)),
             dma, dma((PIECES,)),
             dma, dma((REPS,)),
             dma, dma((REPS,)),
-            dma((2,)), dma((2, 2)),
-            dma((2,)), dma((2, NZ)),
-            dma((2,)), dma((2, 2 * REACH - 1)), dma((2, 2 * REACH)),
+            dma((3,)), dma((3, 2)),
+            dma((3,)), dma((3, NZ)),
+            dma((3,)), dma((3, 2 * REACH - 1)), dma((3, 2 * REACH)),
         ],
         compiler_params=pltpu.CompilerParams(
             collective_id=0, has_side_effects=True, vmem_limit_bytes=56 * 1024 * 1024

time: 70.1 us -> 68.2 us (0.973)
  local copies, waits for them, and re-layouts: 1.4 us -> 0.62 us
    unnamed x1, local copies, waits for them, and re-layouts: 1.4 us -> 0.62 us
    pallas_call x1, Pallas kernels: 68.1 us -> 67.4 us  [per_device(): pl.pallas_call(kernel, out_shape=pltpu.VMEM((ROWS, OUTC), F32), in_specs=...]
where the time goes in v3:
time: 68.2 us; the launch traced here: 68 us
  Pallas kernels  67.4 us (99%)
    pallas_call x1, Pallas kernels, per_device(): pl.pallas_call(kernel, out_shape=pltpu.VMEM((ROWS, OUTC), F32), in_specs=...  67.4 us

profile of v3, /device:TPU:24, one launch (start us, length us, event | category | flops | bytes accessed | tf_op | source)
XLA Modules:
  0.0 68.0 jit_solution(13633072253507130291)
XLA Ops:
  0.0 67.4 %shard_map.73 = f32[7,1280]{1,0:T(8,128)S(1)} custom-call(bf16[256,3584]{1,0:T(8,128)(2,1)} %x_hbm.1, bf16[256,3584]{1,0:T(8,128)(2,1)} %y_hbm.1, bf16[7,768]{1,0:T(8,128)(2,1)} %wqkv_hbm.1, bf16[7,512]{1,0:T(8,128)(2,1)} %wo_hbm.1, s32[1,256]{1,0:T(1,128)} %lab_hbm.1, bf16[1,256,4,256]{3,2,1,0:T(4,128)(2,1)} %noise_hbm.1, s32[1,8]{1,0:T(1,128)} %bitcast.1), custom_call_target="tpu_custom_call" | custom-call | tf_op jit(solution)/shard_map/pallas_call | solution.py:497
  67.4 0.6 copy.9

commit v4 on v3

--- a/solution.py
+++ b/solution.py
@@ -37,7 +37,6 @@
     nhi, nband, nrecv, nstage, nfull, prj, kvp, kv_ref, allow,
     g_0, gs_0, r1_0, s2_0, r2_0, acc_0, s3_0, relay_0, fin_0,
     g_1, gs_1, r1_1, s2_1, r2_1, acc_1, s3_1, relay_1, fin_1,
-    g_2, gs_2, r1_2, s2_2, r2_2, acc_2, s3_2, relay_2, fin_2,
     loc, p0_send, p0_recv, nz_send, nz_recv, nf_send, nf_recv, w_send, w_recv,
     kv_send, kv_recv, pr_send, pr_recv,
     r1_send, r1_recv, r2_send, r2_recv, r3_send, relay_recv, fin_recv,
@@ -50,8 +49,10 @@
     partner = grp + 1 - 2 * core
     beside = grp + 32 - 64 * x_lo
 
+    way = 1 - 2 * core
+
     def along(d):
-        return lax.rem(z + (d + NZ), NZ)
+        return lax.rem(z + way * d + NZ, NZ)
 
     def at_z(zz):
         return x_lo * 32 + zz * 2 + core
@@ -164,16 +165,16 @@
         s = mate(k)
         rcopy(p0s.at[s], p0r.at[s], p0_send, p0_recv.at[s], s, grp).wait_recv()
     for t in range(4):
-        wbuf[t, grp, 0:8] = p0r[2 * t, 0]
-        wbuf[t, grp, 8:16] = p0r[2 * t + 1, 0]
+        wbuf[grp, t, 0:8] = p0r[2 * t, 0]
+        wbuf[grp, t, 8:16] = p0r[2 * t + 1, 0]
     for half in range(2):
         total = p0r[half, 1].astype(F32)
         for b in range(1, 4):
             total = total + p0r[2 * b + half, 1].astype(F32)
-        wbuf[4, grp, 8 * half : 8 * half + 8] = total.astype(BF)
+        wbuf[grp, 4, 8 * half : 8 * half + 8] = total.astype(BF)
 
     def piece(p, g):
-        return rcopy(wbuf.at[:, p], wbuf.at[:, p], w_send, w_recv.at[p], rep, g)
+        return rcopy(wbuf.at[p], wbuf.at[p], w_send, w_recv.at[p], rep, g)
 
     for d in near:
         piece(grp, at_z(along(d))).start()
@@ -255,7 +256,7 @@
     lane = iota((SEQ, HD), 1) // 32
 
     def kv_part(side):
-        w = wbuf[4, pl.ds(side * 32, 32)].reshape(512, HD)
+        w = wbuf[pl.ds(side * 32, 32), 4].reshape(512, HD)
         lanes = pl.ds(pl.multiple_of(512 * side, 128), 512)
         total = jnp.zeros((SEQ, HD), F32)
         for b in range(4):
@@ -266,7 +267,7 @@
         lanes = pl.ds(pl.multiple_of(512 * side, 128), 512)
         total = jnp.zeros((SEQ, HD), F32)
         for t in range(4):
-            total = total + dot(ze[t, :, lanes], wbuf[t, pl.ds(side * 32, 32)].reshape(512, HD))
+            total = total + dot(ze[t, :, lanes], wbuf[pl.ds(side * 32, 32), t].reshape(512, HD))
         return total
 
     from_partner(x_lo)
@@ -333,7 +334,7 @@
 
     heads = [lax.rem(rep + o, HQ) for o in (0, 1, 3, 2)]
 
-    place = ((g_0, 0), (g_1, 0), (g_1, 2), (g_2, 0))
+    place = ((g_0, 0), (g_0, 2), (g_0, 4), (g_1, 0))
 
     def attend(i, key_grad, val_grad):
         h = heads[i]
@@ -442,36 +443,29 @@
 
     one = Sums(0, g_0, gs_0, r1_0, s2_0, r2_0, acc_0, s3_0, relay_0, fin_0)
     two = Sums(1, g_1, gs_1, r1_1, s2_1, r2_1, acc_1, s3_1, relay_1, fin_1)
-    three = Sums(2, g_2, gs_2, r1_2, s2_2, r2_2, acc_2, s3_2, relay_2, fin_2)
-
-    key_grad, val_grad = attend(0, key_grad, val_grad)
+    for i in range(3):
+        key_grad, val_grad = attend(i, key_grad, val_grad)
     one.to_partner()
-    key_grad, val_grad = attend(1, key_grad, val_grad)
     one.to_beside()
-    key_grad, val_grad = attend(2, key_grad, val_grad)
+    key_grad, val_grad = attend(3, key_grad, val_grad)
+    put(g_1, 2, dot(xo_t[...], key_grad.astype(BF)))
+    put(g_1, 3, dot(xo_t[...], val_grad.astype(BF)))
     two.to_partner()
     one.to_z()
     two.to_beside()
-    key_grad, val_grad = attend(3, key_grad, val_grad)
-    put(g_2, 2, dot(xo_t[...], key_grad.astype(BF)))
-    put(g_2, 3, dot(xo_t[...], val_grad.astype(BF)))
-    three.to_partner()
     two.to_z()
-    three.to_beside()
     one.relays()
-    three.to_z()
     two.relays()
-    three.relays()
 
     def write(total, at, lanes):
         out_ref[:, lanes] = total[0:ROWS, 128 * at : 128 * at + 128]
 
-    finals = {id(g.g32): g.final() for g in (one, two, three)}
+    finals = {id(g.g32): g.final() for g in (one, two)}
     for i, (g32, at) in enumerate(place):
         write(finals[id(g32)], at, pl.ds(pl.multiple_of(128 * heads[i], 128), 128))
         write(finals[id(g32)], at + 1, pl.ds(pl.multiple_of(768 + 128 * heads[i], 128), 128))
-    write(finals[id(g_2)], 2, pl.ds(512, 128))
-    write(finals[id(g_2)], 3, pl.ds(640, 128))
+    write(finals[id(g_1)], 2, pl.ds(512, 128))
+    write(finals[id(g_1)], 3, pl.ds(640, 128))
 
     def sent(ref, sem):
         pltpu.make_async_copy(ref, ref, sem).wait()
@@ -480,10 +474,10 @@
     sent(nrecv.at[pl.ds(0, 7)], nz_send)
     for k in range(1, REPS):
         rcopy(nstage, nfull.at[:, rows_own], nf_send, nf_recv.at[rep], mate(k), grp).wait_send()
-    sent(wbuf.at[:, pl.ds(0, 63)], w_send)
+    sent(wbuf.at[pl.ds(0, 63)], w_send)
     sent(kvp.at[pl.ds(0, 7)], kv_send)
     sent(prj.at[pl.ds(0, 7)], pr_send)
-    for g in (one, two, three):
+    for g in (one, two):
         sent(g.gs, r1_send.at[g.n])
         sent(g.s2, r2_send.at[g.n])
         sent(g.s3.at[pl.ds(0, 15)], r3_send.at[g.n])
@@ -515,7 +509,7 @@
             vm((512, SEQ), BF),
             vm((REPS, 2, 8, 128), BF),
             vm((REPS, 2, 8, 128), BF),
-            vm((5, PIECES, 16, 128), BF),
+            vm((PIECES, 5, 16, 128), BF),
             vm((128, HQ, SEQ), BF),
             vm((SEQ, HQ, 128), BF),
             vm((REPS, 32, HQ, 128), BF),
@@ -528,7 +522,7 @@
         ]
         + [
             s
-            for width in (256, 512, 512)
+            for width in (768, 512)
             for s in (
                 vm((PIECES, 8, width), F32),
                 vm((2, NZ, 8, width), BF),
@@ -549,9 +543,9 @@
             dma, dma((PIECES,)),
             dma, dma((REPS,)),
             dma, dma((REPS,)),
-            dma((3,)), dma((3, 2)),
-            dma((3,)), dma((3, NZ)),
-            dma((3,)), dma((3, 2 * REACH - 1)), dma((3, 2 * REACH)),
+            dma((2,)), dma((2, 2)),
+            dma((2,)), dma((2, NZ)),
+            dma((2,)), dma((2, 2 * REACH - 1)), dma((2, 2 * REACH)),
         ],
         compiler_params=pltpu.CompilerParams(
             collective_id=0, has_side_effects=True, vmem_limit_bytes=56 * 1024 * 1024

time: 68.2 us -> 67.6 us (level)
  no operation moved by 1% of the time
where the time goes in v4:
time: 67.6 us; the launch traced here: 67.4 us
  Pallas kernels  66.8 us (99%)
    pallas_call x1, Pallas kernels, per_device(): pl.pallas_call(kernel, out_shape=pltpu.VMEM((ROWS, OUTC), F32), in_specs=...  66.8 us

profile of v4, /device:TPU:24, one launch (start us, length us, event | category | flops | bytes accessed | tf_op | source)
XLA Modules:
  0.0 67.4 jit_solution(1129338302600378073)
XLA Ops:
  0.0 66.8 %shard_map.73 = f32[7,1280]{1,0:T(8,128)S(1)} custom-call(bf16[256,3584]{1,0:T(8,128)(2,1)} %x_hbm.1, bf16[256,3584]{1,0:T(8,128)(2,1)} %y_hbm.1, bf16[7,768]{1,0:T(8,128)(2,1)} %wqkv_hbm.1, bf16[7,512]{1,0:T(8,128)(2,1)} %wo_hbm.1, s32[1,256]{1,0:T(1,128)} %lab_hbm.1, bf16[1,256,4,256]{3,2,1,0:T(4,128)(2,1)} %noise_hbm.1, s32[1,8]{1,0:T(1,128)} %bitcast.1), custom_call_target="tpu_custom_call" | custom-call | tf_op jit(solution)/shard_map/pallas_call | solution.py:491
  66.8 0.6 copy.9

commit v5 on v4

--- a/solution.py
+++ b/solution.py
@@ -263,16 +263,16 @@
             total = jnp.where(lane == b, dot(xe[b, :, lanes], w), total)
         return total
 
-    def own_part(side):
+    def own_part(side, rows):
         lanes = pl.ds(pl.multiple_of(512 * side, 128), 512)
-        total = jnp.zeros((SEQ, HD), F32)
+        total = jnp.zeros((rows.stop - rows.start, HD), F32)
         for t in range(4):
-            total = total + dot(ze[t, :, lanes], wbuf[pl.ds(side * 32, 32), t].reshape(512, HD))
+            total = total + dot(ze[t, rows, lanes], wbuf[pl.ds(side * 32, 32), t].reshape(512, HD))
         return total
 
     from_partner(x_lo)
     kv_sum = kv_part(x_lo)
-    own_cols = own_part(x_lo)
+    own_cols = own_part(x_lo, slice(0, SEQ))
     from_partner(1 - x_lo)
     kv_sum = kv_sum + kv_part(1 - x_lo)
     kv_sum = kv_sum + pltpu.roll(kv_sum, 64, 1)
@@ -285,10 +285,15 @@
     far_first = (2, 6, 1, 3, 5, 7, 4)
     for k in far_first:
         rcopy(kvp.at[rep], kvp.at[rep], kv_send, kv_recv.at[rep], mate(k), grp).start()
-    own_cols = own_cols + own_part(1 - x_lo)
-    prj[rep] = own_cols.astype(BF)
-    for k in (4, 1, 3, 5, 7, 2, 6):
-        rcopy(prj.at[rep], prj.at[rep], pr_send, pr_recv.at[rep], mate(k), grp).start()
+    def columns(r, half, g):
+        rows = prj.at[r, pl.ds(128 * half, 128)]
+        return rcopy(rows, rows, pr_send, pr_recv.at[half, r], g, grp)
+
+    for half in range(2):
+        rows = slice(128 * half, 128 * half + 128)
+        prj[rep, rows] = (own_cols[rows] + own_part(1 - x_lo, rows)).astype(BF)
+        for k in (4, 1, 3, 5, 7, 2, 6):
+            columns(rep, half, mate(k)).start()
 
     crow = iota((512, 128), 0)
     pidx = crow // 8
@@ -339,11 +344,12 @@
     def attend(i, key_grad, val_grad):
         h = heads[i]
         if i == 0:
-            s = mate(HQ)
-            rcopy(prj.at[s], prj.at[s], pr_send, pr_recv.at[s], s, grp).wait_recv()
+            for half in range(2):
+                columns(mate(HQ), half, mate(HQ)).wait_recv()
         else:
             for s in (h, HQ + h):
-                rcopy(prj.at[s], prj.at[s], pr_send, pr_recv.at[s], s, grp).wait_recv()
+                for half in range(2):
+                    columns(s, half, s).wait_recv()
         q, a = prj[h], prj[HQ + h]
         scores = dot(q, keys, ((1,), (1,))) * scale
         scores = jnp.where(allow[...] > 0.5, scores, -jnp.inf)
@@ -401,11 +407,12 @@
 
         def to_beside(self):
             self.core_copy(0).wait_recv()
-            self.s2[...] = (
-                self.g32[pl.ds(mine + (1 - x_lo) * 16, 16)] + self.r1[0].astype(F32)
-            ).astype(BF)
             for d in order:
-                self.cross(along(d)).start()
+                zz = along(d)
+                self.s2[zz] = (
+                    self.g32[mine + (1 - x_lo) * 16 + zz] + self.r1[0, zz].astype(F32)
+                ).astype(BF)
+                self.cross(zz).start()
             self.core_copy(1).wait_recv()
             self.acc[...] = self.g32[pl.ds(mine + x_lo * 16, 16)] + self.r1[1].astype(F32)
 
@@ -542,7 +549,7 @@
             dma, dma((REPS,)),
             dma, dma((PIECES,)),
             dma, dma((REPS,)),
-            dma, dma((REPS,)),
+            dma, dma((2, REPS)),
             dma((2,)), dma((2, 2)),
             dma((2,)), dma((2, NZ)),
             dma((2,)), dma((2, 2 * REACH - 1)), dma((2, 2 * REACH)),

time: 67.6 us -> 67.8 us (level)
  no operation moved by 1% of the time
where the time goes in v5:
time: 67.8 us; the launch traced here: 67.5 us
  Pallas kernels  66.8 us (99%)
    pallas_call x1, Pallas kernels, per_device(): pl.pallas_call(kernel, out_shape=pltpu.VMEM((ROWS, OUTC), F32), in_specs=...  66.8 us

profile of v5, /device:TPU:24, one launch (start us, length us, event | category | flops | bytes accessed | tf_op | source)
XLA Modules:
  0.0 67.5 jit_solution(3943927924752532589)
XLA Ops:
  0.0 66.8 %shard_map.73 = f32[7,1280]{1,0:T(8,128)S(1)} custom-call(bf16[256,3584]{1,0:T(8,128)(2,1)} %x_hbm.1, bf16[256,3584]{1,0:T(8,128)(2,1)} %y_hbm.1, bf16[7,768]{1,0:T(8,128)(2,1)} %wqkv_hbm.1, bf16[7,512]{1,0:T(8,128)(2,1)} %wo_hbm.1, s32[1,256]{1,0:T(1,128)} %lab_hbm.1, bf16[1,256,4,256]{3,2,1,0:T(4,128)(2,1)} %noise_hbm.1, s32[1,8]{1,0:T(1,128)} %bitcast.1), custom_call_target="tpu_custom_call" | custom-call | tf_op jit(solution)/shard_map/pallas_call | solution.py:498
  66.9 0.6 copy.9
